TPU v7x, 512 devices: a whole 4x4x16 slice. The times are simulated.
512 devices in a mesh: depth: 32 (over y, x, core), tile: 16 (over z).
Axes of the slice: x: 4, y: 4, z: 16, core: 2. Of those that a mesh axis runs over, the one named last changes fastest.
Arguments:
- field: float32 [128, 1536, 1024], P('depth', 'tile'), may hold values from -6 to 6
Outputs:
- image: float32 [4, 1536, 1024], P(None, ('tile', 'depth'))
All inputs are finite; a program needn't handle non-finite values.
Results may differ from a plain program's by a relative error of at most 0.0003.
Values sent between devices are 32-bit elements; how exact they have to be, the bound alone decides.
No kernel may reach another device: no remote copies, remote signals or barrier semaphores. Data moves between devices by JAX's collectives and lax.ppermute only.
A program may use at most 64 MiB of HBM per device.

v0:
```python
import jax
import jax.numpy as jnp
from jax import lax
from jax.sharding import PartitionSpec as P

centres = (-1.2, 0.3, 1.5)
spreads = (0.25, 0.35, 0.3)
heights = (2.0, 1.0, 3.0)
floor_density = 0.05
light_cols = 0.48
light_rows = 0.6
light_depth = 0.64


def from_behind(block, axis, distance):
    devices = range(lax.axis_size(axis))
    route = [(i - distance, i) for i in devices if i - distance in devices]
    return lax.ppermute(block, axis, route)


def extended(cells, sides, width):
    for axis, dim in sides:
        count = lax.axis_size(axis)
        ends = count - 1
        head = lax.slice_in_dim(cells, 0, width, axis=dim)
        tail = lax.slice_in_dim(cells, cells.shape[dim] - width, cells.shape[dim], axis=dim)
        cells = jnp.concatenate(
            [
                lax.ppermute(tail, axis, [(i, (i + 1) % count) for i in range(ends)]),
                cells,
                lax.ppermute(head, axis, [((i + 1) % count, i) for i in range(ends)]),
            ],
            axis=dim,
        )
    return cells


def emission(sample, slope_cols, slope_rows, slope_depth):
    density = floor_density + jnp.zeros_like(sample)
    for centre, spread, bump_height in zip(centres, spreads, heights):
        scaled = (sample - centre) / spread
        density = density + bump_height * jnp.exp(-scaled * scaled)
    facing = light_cols * slope_cols + light_rows * slope_rows + light_depth * slope_depth
    length = slope_cols * slope_cols + slope_rows * slope_rows + slope_depth * slope_depth + 1.0
    shading = 0.3 + 0.7 * jnp.abs(facing) * lax.rsqrt(length)
    colour = jnp.stack(
        [
            shading * jax.nn.sigmoid(2.0 * sample),
            shading * jnp.exp(-sample * sample),
            shading * jax.nn.sigmoid(-2.0 * sample),
        ]
    )
    return (density, colour)


def integrate(density, colour, spacing):
    optics = spacing * density
    running = jnp.cumsum(optics, axis=0)
    before = jnp.concatenate([jnp.zeros_like(optics[:1]), running[:-1]], axis=0)
    weight = jnp.exp(-before) * -jnp.expm1(-optics)
    return (jnp.sum(weight[None] * colour, axis=1), jnp.exp(-running[-1]))


def blend_all(pieces):
    colour_in, through_in = pieces
    passed = jnp.cumprod(through_in, axis=1)
    before = jnp.concatenate([jnp.ones_like(through_in[:, :1]), passed[:, :-1]], axis=1)
    return (jnp.sum(before * colour_in, axis=1), passed[:, -1])


def local(field):
    planes, row_count, col_count = field.shape
    depth_count = lax.axis_size("depth")
    spacing = 3.0 / (planes * depth_count)
    following = from_behind(field[:1], "depth", -1)
    further = jnp.concatenate([field[1:], following], axis=0)
    sample = 0.5 * (field + further)
    slope_depth = further - field
    edge_rows = jnp.concatenate([sample[:, :1], sample[:, -1:]], axis=1)
    edge_padded = extended(edge_rows, (("tile", 1),), 1)
    padded = jnp.concatenate([edge_padded[:, :1], sample, edge_padded[:, -1:]], axis=1)
    slope_rows = 0.5 * (padded[:, 2:] - padded[:, :-2])
    zero_col = jnp.zeros_like(sample[..., :1])
    slope_cols = 0.5 * (
        jnp.concatenate([sample[..., 1:], zero_col], axis=-1)
        - jnp.concatenate([zero_col, sample[..., :-1]], axis=-1)
    )
    density, colour = emission(sample, slope_cols, slope_rows, slope_depth)
    colour_sum, through = integrate(density, colour, spacing)
    row_share = row_count // depth_count
    colour_parts = colour_sum.reshape(3, depth_count, row_share, col_count)
    through_parts = through.reshape(1, depth_count, row_share, col_count)
    colour_out, through_out = blend_all(
        (
            lax.all_to_all(colour_parts, "depth", split_axis=1, concat_axis=1, tiled=True),
            lax.all_to_all(through_parts, "depth", split_axis=1, concat_axis=1, tiled=True),
        )
    )
    return jnp.concatenate([colour_out, 1.0 - through_out], axis=0)


def solution(mesh):
    return jax.shard_map(
        local,
        mesh=mesh,
        in_specs=(P("depth", "tile", None),),
        out_specs=P(None, ("tile", "depth"), None),
        check_vma=False,
    )
```

profile of v0, /device:TPU:96, one launch (start us, length us, event | category | flops | bytes accessed | tf_op | source)
XLA Modules:
  0.0 78.3 jit_solution(17771362351667191256)
XLA Ops:
  0.0 0.0 copy-start
  0.0 1.1 %slice.39 = f32[1,96,1024]{2,1,0:T(8,128)S(1)} slice(f32[4,96,1024]{2,1,0:T(8,128)} %param.1), slice={[0:1], [0:96], [0:1024]} | slice | bytes 786432 | tf_op jit(solution)/shard_map/slice | solution.py:75
  1.1 1.3 %collective-permute-start = (f32[1,96,1024]{2,1,0:T(8,128)S(1)}, f32[1,96,1024]{2,1,0:T(8,128)S(1)}, u32[]{:S(2)}, u32[]{:S(2)}) collective-permute-start(f32[1,96,1024]{2,1,0:T(8,128)S(1)} %slice.39), channel_id=1, source_target_pairs={{16,0},{32,16},{48,32},{64,48},{80,64},{96,80},{112,96},{128,112},... | collective-permute-start | bytes 1179656 | tf_op jit(solution)/shard_map/ppermute | solution.py:18
  2.4 1.4 %slice.38 = f32[3,96,1024]{2,1,0:T(8,128)S(1)} slice(f32[4,96,1024]{2,1,0:T(8,128)} %param.1), slice={[1:4], [0:96], [0:1024]} | slice | bytes 2359296 | tf_op jit(solution)/shard_map/slice | solution.py:76
  3.8 0.0 copy-start.1
  3.8 1.0 %collective-permute-done = f32[1,96,1024]{2,1,0:T(8,128)S(1)} collective-permute-done((f32[1,96,1024]{2,1,0:T(8,128)S(1)}, f32[1,96,1024]{2,1,0:T(8,128)S(1)}, u32[]{:S(2)}, u32[]{:S(2)}) %collective-permute-start) | collective-permute-done | bytes 393248 | tf_op jit(solution)/shard_map/ppermute | solution.py:18
  4.8 0.0 copy-done
  4.8 0.3 broadcast_multiply_fusion
  5.1 0.0 copy-done.1
  5.1 2.3 %fusion.22 = (f32[4,96,1023]{2,1,0:T(8,128)}, f32[4,96,1023]{2,1,0:T(8,128)}) fusion(f32[4,96,1024]{2,1,0:T(8,128)S(1)} %get-tuple-element.7), kind=kLoop, calls=%fused_computation.38 | loop fusion | bytes 6285312 | tf_op jit(solution)/shard_map/slice | solution.py:85
  7.4 0.6 fusion.23
  8.0 2.0 %collective-permute-start.1 = (f32[4,1,1024]{2,1,0:T(1,128)}, f32[4,1,1024]{2,1,0:T(1,128)S(1)}, u32[]{:S(2)}, u32[]{:S(2)}) collective-permute-start(f32[4,1,1024]{2,1,0:T(1,128)} %get-tuple-element.14), channel_id=1, source_target_pairs={{1,0},{2,1},{3,2},{4,3},{5,4},{6,5},{7,6},{8,7},{9,8},{10,9},{11,1... | collective-permute-start | bytes 49160 | tf_op jit(solution)/shard_map/ppermute | solution.py:31
  10.0 5.0 %collective-permute-start.2 = (f32[4,1,1024]{2,1,0:T(1,128)}, f32[4,1,1024]{2,1,0:T(1,128)}, u32[]{:S(2)}, u32[]{:S(2)}) collective-permute-start(f32[4,1,1024]{2,1,0:T(1,128)} %get-tuple-element.15), channel_id=1, source_target_pairs={{0,1},{1,2},{2,3},{3,4},{4,5},{5,6},{6,7},{7,8},{8,9},{9,10},{10,1... | collective-permute-start | bytes 49160 | tf_op jit(solution)/shard_map/ppermute | solution.py:29
  15.1 1.5 %fusion.19 = f32[4,96,1024]{2,1,0:T(8,128)S(1)} fusion(f32[4,96,1024]{2,1,0:T(8,128)S(1)} %get-tuple-element.8), kind=kOutput, calls=%fused_computation.37 | output fusion | flops 8650752 | bytes 3145728 | tf_op jit(solution)/shard_map/jit(cumsum)/reduce_window_sum | solution.py:58
  16.6 0.8 %fusion.17 = f32[1,96,1024]{2,1,0:T(8,128)} fusion(f32[4,96,1024]{2,1,0:T(8,128)S(1)} %fusion.19), kind=kLoop, calls=%fused_computation.33 | loop fusion | flops 98304 | bytes 786432 | tf_op jit(solution)/shard_map/exp | solution.py:61
  17.4 1.1 %slice.52 = f32[3,96,1024]{2,1,0:T(8,128)} slice(f32[4,96,1024]{2,1,0:T(8,128)S(1)} %fusion.19), slice={[0:3], [0:96], [0:1024]} | slice | bytes 2359296 | tf_op jit(solution)/shard_map/slice | solution.py:59
  18.5 2.2 %exp.38 = f32[1,32,3,1024]{3,0,2,1:T(1,128)} reshape(f32[1,96,1024]{2,1,0:T(8,128)} %fusion.17) | data formatting | bytes 786432 | tf_op jit(solution)/shard_map/exp | solution.py:61
  20.7 13.8 %all-to-all-start = ((f32[1,32,3,1024]{3,0,2,1:T(1,128)}), f32[1,32,3,1024]{3,0,2,1:T(1,128)}, u32[]{:S(2)}, u32[]{:S(2)}) async-start(f32[1,32,3,1024]{3,0,2,1:T(1,128)} %exp.38), calls=%async_computation | async-start | bytes 786432 | tf_op jit(solution)/shard_map/all_to_all | solution.py:96
  34.5 0.0 collective-permute-done.1
  34.5 0.0 collective-permute-done.2
  34.6 0.0 copy-start.2
  34.6 4.0 %multiply_bitcast_fusion.1 = (f32[1,4,96,1024]{3,2,1,0:T(8,128)S(1)}, f32[4,96,1024]{2,1,0:T(8,128)S(1)}) fusion(f32[4,96,1024]{2,1,0:T(8,128)S(1)} %get-tuple-element.8, f32[4,96,1024]{2,1,0:T(8,128)} %param.1, f32[1,96,1024]{2,1,0:T(8,128)S(1)} %collective-permute-done, f32[3,96,1024]{2,1,0:T(8,128)} %copy-done.1, f32[4,96,1024]{2,1,0:T(8,128)S(1)} %get-tuple-element.7, ...), kind=kLoop, calls=%fused_computation.24 | loop fusion | flops 10616832 | bytes 12612608 | tf_op jit(solution)/shard_map/stack | solution.py:46
  38.5 0.0 copy-done.2
  38.5 2.4 %fusion.12 = (f32[1,4,96,1024]{3,2,1,0:T(8,128)S(1)}, f32[1,4,96,1024]{3,2,1,0:T(8,128)S(1)}, f32[4,96,1024]{2,1,0:T(8,128)S(1)}) fusion(f32[4,96,1024]{2,1,0:T(8,128)S(1)} %get-tuple-element.6, f32[4,96,1024]{2,1,0:T(8,128)S(1)} %get-tuple-element.8, f32[3,96,1024]{2,1,0:T(8,128)S(1)} %copy-done.2), kind=kLoop, calls=%fused_computation.17 | loop fusion | flops 12189696 | bytes 9043968 | tf_op jit(solution)/shard_map/stack | solution.py:46
  40.9 1.9 %fusion = f32[3,96,1024]{2,1,0:T(8,128)} fusion(f32[1,4,96,1024]{3,2,1,0:T(8,128)S(1)} %get-tuple-element.10, f32[1,4,96,1024]{3,2,1,0:T(8,128)S(1)} %get-tuple-element.9, f32[1,4,96,1024]{3,2,1,0:T(8,128)S(1)} %get-tuple-element.5, f32[4,96,1024]{2,1,0:T(8,128)S(1)} %get-tuple-element.11), kind=kLoop, calls=%fused_computation.1 | loop fusion | flops 4423680 | bytes 7471104 | tf_op jit(solution)/shard_map/reduce_sum | solution.py:61
  42.8 1.6 %reshape.34 = f32[3,32,3,1024]{3,2,1,0:T(4,128)S(1)} reshape(f32[3,96,1024]{2,1,0:T(8,128)} %fusion) | data formatting | bytes 2359296 | tf_op jit(solution)/shard_map/reshape | solution.py:91
  44.4 1.5 %copy.6 = f32[3,32,3,1024]{3,2,0,1:T(4,128)} copy(f32[3,32,3,1024]{3,2,1,0:T(4,128)S(1)} %reshape.34) | data formatting | bytes 2359296 | tf_op jit(solution)/shard_map/reshape | solution.py:91
  45.8 0.0 all-to-all-done
  45.8 7.3 %all-to-all-start.1 = ((f32[3,32,3,1024]{3,2,0,1:T(4,128)}), f32[3,32,3,1024]{3,2,0,1:T(4,128)S(1)}, u32[]{:S(2)}, u32[]{:S(2)}) async-start(f32[3,32,3,1024]{3,2,0,1:T(4,128)} %copy.6), calls=%async_computation.1 | async-start | bytes 3145728 | tf_op jit(solution)/shard_map/all_to_all | solution.py:95
  53.2 1.1 %fusion.15 = f32[1,32,3,1024]{3,2,1,0:T(4,128)S(1)} fusion(f32[1,32,3,1024]{3,0,2,1:T(1,128)} %all-to-all-done), kind=kOutput, calls=%fused_computation.29 | output fusion | flops 3047424 | bytes 786432 | tf_op jit(solution)/shard_map/jit(cumprod)/reduce_window | solution.py:66
  54.3 0.1 slice.51
  54.4 0.1 pad_bitcast_fusion
  54.6 22.5 %all-to-all-done.1 = f32[3,32,3,1024]{3,2,0,1:T(4,128)S(1)} async-done(((f32[3,32,3,1024]{3,2,0,1:T(4,128)}), f32[3,32,3,1024]{3,2,0,1:T(4,128)S(1)}, u32[]{:S(2)}, u32[]{:S(2)}) %all-to-all-start.1) | async-done | bytes 1179680 | tf_op jit(solution)/shard_map/all_to_all | solution.py:95
  77.1 0.5 multiply_reduce_fusion
  77.6 0.7 copy.8
  (2 shorter events, 0.0 us)
Async XLA Ops:
  0.0 4.8 %copy-start = (f32[4,96,1024]{2,1,0:T(8,128)S(1)}, f32[4,96,1024]{2,1,0:T(8,128)}, u32[]{:S(2)}) copy-start(f32[4,96,1024]{2,1,0:T(8,128)} %param.1) | copy-start | bytes 4718596
  1.1 3.6 %collective-permute-start = (f32[1,96,1024]{2,1,0:T(8,128)S(1)}, f32[1,96,1024]{2,1,0:T(8,128)S(1)}, u32[]{:S(2)}, u32[]{:S(2)}) collective-permute-start(f32[1,96,1024]{2,1,0:T(8,128)S(1)} %slice.39), channel_id=1, source_target_pairs={{16,0},{32,16},{48,32},{64,48},{80,64},{96,80},{112,96},{128,112},... | collective-permute-start | bytes 1179656 | tf_op jit(solution)/shard_map/ppermute | solution.py:18
  3.8 1.3 %copy-start.1 = (f32[3,96,1024]{2,1,0:T(8,128)}, f32[3,96,1024]{2,1,0:T(8,128)S(1)}, u32[]{:S(2)}) copy-start(f32[3,96,1024]{2,1,0:T(8,128)S(1)} %slice.38) | copy-start | bytes 3538948
  8.0 26.5 %collective-permute-start.1 = (f32[4,1,1024]{2,1,0:T(1,128)}, f32[4,1,1024]{2,1,0:T(1,128)S(1)}, u32[]{:S(2)}, u32[]{:S(2)}) collective-permute-start(f32[4,1,1024]{2,1,0:T(1,128)} %get-tuple-element.14), channel_id=1, source_target_pairs={{1,0},{2,1},{3,2},{4,3},{5,4},{6,5},{7,6},{8,7},{9,8},{10,9},{11,1... | collective-permute-start | bytes 49160 | tf_op jit(solution)/shard_map/ppermute | solution.py:31
  10.0 24.5 %collective-permute-start.2 = (f32[4,1,1024]{2,1,0:T(1,128)}, f32[4,1,1024]{2,1,0:T(1,128)}, u32[]{:S(2)}, u32[]{:S(2)}) collective-permute-start(f32[4,1,1024]{2,1,0:T(1,128)} %get-tuple-element.15), channel_id=1, source_target_pairs={{0,1},{1,2},{2,3},{3,4},{4,5},{5,6},{6,7},{7,8},{8,9},{9,10},{10,1... | collective-permute-start | bytes 49160 | tf_op jit(solution)/shard_map/ppermute | solution.py:29
  20.7 25.1 %all-to-all-start = ((f32[1,32,3,1024]{3,0,2,1:T(1,128)}), f32[1,32,3,1024]{3,0,2,1:T(1,128)}, u32[]{:S(2)}, u32[]{:S(2)}) async-start(f32[1,32,3,1024]{3,0,2,1:T(1,128)} %exp.38), calls=%async_computation | async-start | bytes 786432 | tf_op jit(solution)/shard_map/all_to_all | solution.py:96
  34.6 4.0 %copy-start.2 = (f32[3,96,1024]{2,1,0:T(8,128)S(1)}, f32[3,96,1024]{2,1,0:T(8,128)}, u32[]{:S(2)}) copy-start(f32[3,96,1024]{2,1,0:T(8,128)} %slice.52) | copy-start | bytes 3538948
  45.8 31.2 %all-to-all-start.1 = ((f32[3,32,3,1024]{3,2,0,1:T(4,128)}), f32[3,32,3,1024]{3,2,0,1:T(4,128)S(1)}, u32[]{:S(2)}, u32[]{:S(2)}) async-start(f32[3,32,3,1024]{3,2,0,1:T(4,128)} %copy.6), calls=%async_computation.1 | async-start | bytes 3145728 | tf_op jit(solution)/shard_map/all_to_all | solution.py:95
where the time goes:
time: 78.7 us; the launch traced here: 78.3 us
  starting transfers between devices  29.5 us (37%)
  waiting for transfers between devices  23.5 us (30%)
  local copies, waits for them, and re-layouts  12.6 us (16%)
  other arithmetic  12.5 us (16%)
    all_to_all x1, waiting for transfers between devices, local(): lax.all_to_all(colour_parts, 'depth', split_axis=1, concat_axis=1, tiled=...  22.5 us
    all_to_all x1, starting transfers between devices, local(): lax.all_to_all(through_parts, 'depth', split_axis=1, concat_axis=1, tiled...  13.8 us
    all_to_all x1, starting transfers between devices, local(): lax.all_to_all(colour_parts, 'depth', split_axis=1, concat_axis=1, tiled=...  7.32 us
    another operation x2, other arithmetic, emission(): jnp.stack([shading * jax.nn.sigmoid(2.0 * sample), shading * jnp.exp(-sam...  6.33 us
    ppermute x1, starting transfers between devices, extended(): lax.ppermute(tail, axis, [(i, (i + 1) % count) for i in range(ends)])  5.04 us
    reshape x2, local copies, waits for them, and re-layouts, local(): colour_parts = colour_sum.reshape(3, depth_count, row_share, col_count)  3.05 us
    slice x1, local copies, waits for them, and re-layouts, local(): sample[..., 1:]  2.26 us
    exp x1, local copies, waits for them, and re-layouts, integrate(): return (jnp.sum(weight[None] * colour, axis=1), jnp.exp(-running[-1]))  2.22 us
  transfers between devices with their start and end apart: 5, of which 2 were waited for; matrix products, arithmetic and copies ran while one was open for 25% of the time, Pallas kernels for 0%

commit v1 on v0

--- a/solution.py
+++ b/solution.py
@@ -92,7 +92,15 @@
     through_parts = through.reshape(1, depth_count, row_share, col_count)
     colour_out, through_out = blend_all(
         (
-            lax.all_to_all(colour_parts, "depth", split_axis=1, concat_axis=1, tiled=True),
+            jnp.concatenate(
+                lax.all_to_all(
+                    jnp.stack(jnp.split(colour_parts, lax.axis_size("depth"), axis=1)),
+                    "depth",
+                    0,
+                    0,
+                ),
+                axis=1,
+            ),
             lax.all_to_all(through_parts, "depth", split_axis=1, concat_axis=1, tiled=True),
         )
     )

time: 78.7 us -> 73.3 us (0.931)
  the two profiles are of different devices: /device:TPU:96 before, /device:TPU:1 now
where the time goes in v1:
time: 73.3 us; the launch traced here: 72.8 us
  starting transfers between devices  30.4 us (41%)
  waiting for transfers between devices  16.9 us (23%)
  local copies, waits for them, and re-layouts  13.7 us (19%)
  other arithmetic  11.4 us (16%)
    all_to_all x1, waiting for transfers between devices, local(): lax.all_to_all(jnp.stack(jnp.split(colour_parts, lax.axis_size('depth'),...  16.9 us
    ppermute x1, starting transfers between devices, from_behind(): return lax.ppermute(block, axis, route)  8.75 us
    all_to_all x1, starting transfers between devices, local(): lax.all_to_all(through_parts, 'depth', split_axis=1, concat_axis=1, tiled...  8.41 us
    all_to_all x1, starting transfers between devices, local(): lax.all_to_all(jnp.stack(jnp.split(colour_parts, lax.axis_size('depth'),...  7.38 us
    another operation x2, other arithmetic, emission(): jnp.stack([shading * jax.nn.sigmoid(2.0 * sample), shading * jnp.exp(-sam...  6.33 us
    ppermute x1, starting transfers between devices, extended(): lax.ppermute(tail, axis, [(i, (i + 1) % count) for i in range(ends)])  4.58 us
    another operation x2, local copies, waits for them, and re-layouts, local(): jnp.stack(jnp.split(colour_parts, lax.axis_size('depth'), axis=1))  2.25 us
    slice x1, local copies, waits for them, and re-layouts, local(): sample[..., 1:]  2.22 us
  transfers between devices with their start and end apart: 5, of which 1 were waited for; matrix products, arithmetic and copies ran while one was open for 26% of the time, Pallas kernels for 0%

profile of v1, /device:TPU:1, one launch (start us, length us, event | category | flops | bytes accessed | tf_op | source)
XLA Modules:
  0.0 72.8 jit_solution(812944307918909386)
XLA Ops:
  0.0 0.0 copy-start
  0.0 1.1 %slice.39 = f32[1,96,1024]{2,1,0:T(8,128)S(1)} slice(f32[4,96,1024]{2,1,0:T(8,128)} %param.1), slice={[0:1], [0:96], [0:1024]} | slice | bytes 786432 | tf_op jit(solution)/shard_map/slice | solution.py:75
  1.1 8.7 %collective-permute-start = (f32[1,96,1024]{2,1,0:T(8,128)S(1)}, f32[1,96,1024]{2,1,0:T(8,128)S(1)}, u32[]{:S(2)}, u32[]{:S(2)}) collective-permute-start(f32[1,96,1024]{2,1,0:T(8,128)S(1)} %slice.39), channel_id=1, source_target_pairs={{16,0},{32,16},{48,32},{64,48},{80,64},{96,80},{112,96},{128,112},... | collective-permute-start | bytes 1179656 | tf_op jit(solution)/shard_map/ppermute | solution.py:18
  9.9 1.4 %slice.38 = f32[3,96,1024]{2,1,0:T(8,128)S(1)} slice(f32[4,96,1024]{2,1,0:T(8,128)} %param.1), slice={[1:4], [0:96], [0:1024]} | slice | bytes 2359296 | tf_op jit(solution)/shard_map/slice | solution.py:76
  11.3 0.0 copy-start.1
  11.3 0.0 collective-permute-done
  11.3 0.0 copy-done
  11.3 0.4 broadcast_multiply_fusion
  11.6 0.7 copy-done.1
  12.3 2.2 %fusion.23 = (f32[4,96,1023]{2,1,0:T(8,128)}, f32[4,96,1023]{2,1,0:T(8,128)}) fusion(f32[4,96,1024]{2,1,0:T(8,128)S(1)} %get-tuple-element.7), kind=kLoop, calls=%fused_computation.103 | loop fusion | bytes 6285312 | tf_op jit(solution)/shard_map/slice | solution.py:85
  14.5 0.6 fusion.24
  15.2 1.3 %collective-permute-start.1 = (f32[4,1,1024]{2,1,0:T(1,128)}, f32[4,1,1024]{2,1,0:T(1,128)S(1)}, u32[]{:S(2)}, u32[]{:S(2)}) collective-permute-start(f32[4,1,1024]{2,1,0:T(1,128)} %get-tuple-element.14), channel_id=1, source_target_pairs={{1,0},{2,1},{3,2},{4,3},{5,4},{6,5},{7,6},{8,7},{9,8},{10,9},{11,1... | collective-permute-start | bytes 49160 | tf_op jit(solution)/shard_map/ppermute | solution.py:31
  16.4 4.6 %collective-permute-start.2 = (f32[4,1,1024]{2,1,0:T(1,128)}, f32[4,1,1024]{2,1,0:T(1,128)}, u32[]{:S(2)}, u32[]{:S(2)}) collective-permute-start(f32[4,1,1024]{2,1,0:T(1,128)} %get-tuple-element.15), channel_id=1, source_target_pairs={{0,1},{1,2},{2,3},{3,4},{4,5},{5,6},{6,7},{7,8},{8,9},{9,10},{10,1... | collective-permute-start | bytes 49160 | tf_op jit(solution)/shard_map/ppermute | solution.py:29
  21.0 1.5 %fusion.20 = f32[4,96,1024]{2,1,0:T(8,128)S(1)} fusion(f32[4,96,1024]{2,1,0:T(8,128)S(1)} %get-tuple-element.8), kind=kOutput, calls=%fused_computation.102 | output fusion | flops 8650752 | bytes 3145728 | tf_op jit(solution)/shard_map/jit(cumsum)/reduce_window_sum | solution.py:58
  22.5 0.8 %fusion.18 = f32[1,96,1024]{2,1,0:T(8,128)} fusion(f32[4,96,1024]{2,1,0:T(8,128)S(1)} %fusion.20), kind=kLoop, calls=%fused_computation.34 | loop fusion | flops 98304 | bytes 786432 | tf_op jit(solution)/shard_map/exp | solution.py:61
  23.3 1.1 %slice.52 = f32[3,96,1024]{2,1,0:T(8,128)} slice(f32[4,96,1024]{2,1,0:T(8,128)S(1)} %fusion.20), slice={[0:3], [0:96], [0:1024]} | slice | bytes 2359296 | tf_op jit(solution)/shard_map/slice | solution.py:59
  24.4 2.2 %exp.38 = f32[1,32,3,1024]{3,0,2,1:T(1,128)} reshape(f32[1,96,1024]{2,1,0:T(8,128)} %fusion.18) | data formatting | bytes 786432 | tf_op jit(solution)/shard_map/exp | solution.py:61
  26.6 8.4 %all-to-all-start = ((f32[1,32,3,1024]{3,0,2,1:T(1,128)}), f32[1,32,3,1024]{3,0,2,1:T(1,128)}, u32[]{:S(2)}, u32[]{:S(2)}) async-start(f32[1,32,3,1024]{3,0,2,1:T(1,128)} %exp.38), calls=%async_computation | async-start | bytes 786432 | tf_op jit(solution)/shard_map/all_to_all | solution.py:104
  35.0 0.0 collective-permute-done.1
  35.1 0.0 collective-permute-done.2
  35.1 0.0 copy-start.2
  35.1 4.0 %multiply_bitcast_fusion.1 = (f32[1,4,96,1024]{3,2,1,0:T(8,128)S(1)}, f32[4,96,1024]{2,1,0:T(8,128)S(1)}) fusion(f32[4,96,1024]{2,1,0:T(8,128)S(1)} %get-tuple-element.8, f32[4,96,1024]{2,1,0:T(8,128)} %param.1, f32[1,96,1024]{2,1,0:T(8,128)S(1)} %collective-permute-done, f32[3,96,1024]{2,1,0:T(8,128)} %copy-done.1, f32[4,96,1024]{2,1,0:T(8,128)S(1)} %get-tuple-element.7, ...), kind=kLoop, calls=%fused_computation.23 | loop fusion | flops 10616832 | bytes 12612608 | tf_op jit(solution)/shard_map/stack | solution.py:46
  39.0 0.0 copy-done.2
  39.1 2.4 %fusion.12 = (f32[1,4,96,1024]{3,2,1,0:T(8,128)S(1)}, f32[1,4,96,1024]{3,2,1,0:T(8,128)S(1)}, f32[4,96,1024]{2,1,0:T(8,128)S(1)}) fusion(f32[4,96,1024]{2,1,0:T(8,128)S(1)} %get-tuple-element.6, f32[4,96,1024]{2,1,0:T(8,128)S(1)} %get-tuple-element.8, f32[3,96,1024]{2,1,0:T(8,128)S(1)} %copy-done.2), kind=kLoop, calls=%fused_computation.17 | loop fusion | flops 12189696 | bytes 9043968 | tf_op jit(solution)/shard_map/stack | solution.py:46
  41.4 0.8 %fusion = f32[3,96,1024]{2,1,0:T(8,128)S(1)} fusion(f32[1,4,96,1024]{3,2,1,0:T(8,128)S(1)} %get-tuple-element.10, f32[1,4,96,1024]{3,2,1,0:T(8,128)S(1)} %get-tuple-element.9, f32[1,4,96,1024]{3,2,1,0:T(8,128)S(1)} %get-tuple-element.5, f32[4,96,1024]{2,1,0:T(8,128)S(1)} %get-tuple-element.11), kind=kLoop, calls=%fused_computation.1 | loop fusion | flops 4423680 | bytes 7471104 | tf_op jit(solution)/shard_map/reduce_sum | solution.py:61
  42.3 0.5 reshape.40
  43.6 2.2 %copy.134 = f32[32,3,1,3,1024]{4,2,3,1,0:T(1,128)} copy(f32[32,3,1,3,1024]{4,3,1,2,0:T(4,128)S(1)} %constant_dynamic-update-slice_fusion) | data formatting | bytes 2359296 | tf_op jit(solution)/shard_map/stack | solution.py:97
  45.8 0.0 all-to-all-done
  45.8 7.4 %all-to-all-start.1 = ((f32[32,3,1,3,1024]{4,2,3,1,0:T(1,128)}), f32[32,3,1,3,1024]{4,2,3,1,0:T(1,128)S(1)}, u32[]{:S(2)}, u32[]{:S(2)}) async-start(f32[32,3,1,3,1024]{4,2,3,1,0:T(1,128)} %copy.134), calls=%async_computation.1 | async-start | bytes 2359296 | tf_op jit(solution)/shard_map/all_to_all | solution.py:96
  53.2 1.1 %fusion.16 = f32[1,32,3,1024]{3,2,1,0:T(4,128)S(1)} fusion(f32[1,32,3,1024]{3,0,2,1:T(1,128)} %all-to-all-done), kind=kOutput, calls=%fused_computation.30 | output fusion | flops 3047424 | bytes 786432 | tf_op jit(solution)/shard_map/jit(cumprod)/reduce_window | solution.py:66
  54.3 0.1 slice.51
  54.4 0.1 pad_bitcast_fusion
  54.6 0.2 copy.102
  54.8 16.9 %all-to-all-done.1 = f32[32,3,1,3,1024]{4,2,3,1,0:T(1,128)S(1)} async-done(((f32[32,3,1,3,1024]{4,2,3,1,0:T(1,128)}), f32[32,3,1,3,1024]{4,2,3,1,0:T(1,128)S(1)}, u32[]{:S(2)}, u32[]{:S(2)}) %all-to-all-start.1) | async-done | bytes 1179680 | tf_op jit(solution)/shard_map/all_to_all | solution.py:96
  71.7 0.4 fusion.15
  72.1 0.7 copy.137
  (34 shorter events, 0.6 us)
Async XLA Ops:
  0.0 11.3 %copy-start = (f32[4,96,1024]{2,1,0:T(8,128)S(1)}, f32[4,96,1024]{2,1,0:T(8,128)}, u32[]{:S(2)}) copy-start(f32[4,96,1024]{2,1,0:T(8,128)} %param.1) | copy-start | bytes 4718596
  1.1 10.1 %collective-permute-start = (f32[1,96,1024]{2,1,0:T(8,128)S(1)}, f32[1,96,1024]{2,1,0:T(8,128)S(1)}, u32[]{:S(2)}, u32[]{:S(2)}) collective-permute-start(f32[1,96,1024]{2,1,0:T(8,128)S(1)} %slice.39), channel_id=1, source_target_pairs={{16,0},{32,16},{48,32},{64,48},{80,64},{96,80},{112,96},{128,112},... | collective-permute-start | bytes 1179656 | tf_op jit(solution)/shard_map/ppermute | solution.py:18
  11.3 1.0 %copy-start.1 = (f32[3,96,1024]{2,1,0:T(8,128)}, f32[3,96,1024]{2,1,0:T(8,128)S(1)}, u32[]{:S(2)}) copy-start(f32[3,96,1024]{2,1,0:T(8,128)S(1)} %slice.38) | copy-start | bytes 3538948
  15.2 19.9 %collective-permute-start.1 = (f32[4,1,1024]{2,1,0:T(1,128)}, f32[4,1,1024]{2,1,0:T(1,128)S(1)}, u32[]{:S(2)}, u32[]{:S(2)}) collective-permute-start(f32[4,1,1024]{2,1,0:T(1,128)} %get-tuple-element.14), channel_id=1, source_target_pairs={{1,0},{2,1},{3,2},{4,3},{5,4},{6,5},{7,6},{8,7},{9,8},{10,9},{11,1... | collective-permute-start | bytes 49160 | tf_op jit(solution)/shard_map/ppermute | solution.py:31
  16.4 18.6 %collective-permute-start.2 = (f32[4,1,1024]{2,1,0:T(1,128)}, f32[4,1,1024]{2,1,0:T(1,128)}, u32[]{:S(2)}, u32[]{:S(2)}) collective-permute-start(f32[4,1,1024]{2,1,0:T(1,128)} %get-tuple-element.15), channel_id=1, source_target_pairs={{0,1},{1,2},{2,3},{3,4},{4,5},{5,6},{6,7},{7,8},{8,9},{9,10},{10,1... | collective-permute-start | bytes 49160 | tf_op jit(solution)/shard_map/ppermute | solution.py:29
  26.6 19.2 %all-to-all-start = ((f32[1,32,3,1024]{3,0,2,1:T(1,128)}), f32[1,32,3,1024]{3,0,2,1:T(1,128)}, u32[]{:S(2)}, u32[]{:S(2)}) async-start(f32[1,32,3,1024]{3,0,2,1:T(1,128)} %exp.38), calls=%async_computation | async-start | bytes 786432 | tf_op jit(solution)/shard_map/all_to_all | solution.py:104
  35.1 4.0 %copy-start.2 = (f32[3,96,1024]{2,1,0:T(8,128)S(1)}, f32[3,96,1024]{2,1,0:T(8,128)}, u32[]{:S(2)}) copy-start(f32[3,96,1024]{2,1,0:T(8,128)} %slice.52) | copy-start | bytes 3538948
  45.8 25.9 %all-to-all-start.1 = ((f32[32,3,1,3,1024]{4,2,3,1,0:T(1,128)}), f32[32,3,1,3,1024]{4,2,3,1,0:T(1,128)S(1)}, u32[]{:S(2)}, u32[]{:S(2)}) async-start(f32[32,3,1,3,1024]{4,2,3,1,0:T(1,128)} %copy.134), calls=%async_computation.1 | async-start | bytes 2359296 | tf_op jit(solution)/shard_map/all_to_all | solution.py:96
